TPU v7x, 256 devices: a whole 4x4x8 slice. The times are simulated.
256 devices in a mesh: gx: 8 (over x, z_lo), gy: 8 (over z_hi, core), gz: 4 (over y).
Axes of the slice: x: 4, y: 4, z: 8 (z_hi: 4, z_lo: 2; z = z_hi * 2 + z_lo), core: 2. Of those that a mesh axis runs over, the one named last changes fastest.
Arguments:
- partials: float32 [32, 128, 128, 512], P('gx', None, 'gy', 'gz'), may hold values from -40 to 40
- code_bits: int32 [32, 128], replicated, may hold values from 0 to 1
- group_map: int32 [32], replicated, may hold values from 0 to 31, each once
- velocity: float32 [128, 128, 512], P('gx', 'gy', 'gz'), may hold values from 1.5 to 4.5
Outputs:
- gradient: float32 [128, 128, 512], P('gx', 'gy', 'gz')
- new_model: float32 [128, 128, 512], P('gx', 'gy', 'gz')
Inputs may be any that keep to these rules, and one draw needn't show every extreme that they name: `group_map`: every group of 0 to 31 stands in exactly one slot.
All inputs are finite; a program needn't handle non-finite values.
Results may differ from a plain program's by a relative error of at most 0.0001.
Values sent between devices are 32-bit elements; how exact they have to be, the bound alone decides.
No kernel may reach another device: no remote copies, remote signals or barrier semaphores. Data moves between devices by JAX's collectives and lax.ppermute only.
A program may use at most 64 MiB of HBM per device.

v0:
```python
import jax
import jax.numpy as jnp
from jax import lax
from jax.experimental import pallas as pl
from jax.experimental.pallas import tpu as pltpu
from jax.sharding import Mesh
from jax.sharding import PartitionSpec as P

ITERS = 3
HALO = ITERS
GX = ("gx_0", "gx_1")
GY = ("gy_0", "gy_1")
ALL = GX + GY + ("gz",)

step_length = 0.5
tv_weight = 0.2
dual_step = 0.28
primal_step = 0.28

VMEM = pl.BlockSpec(memory_space=pltpu.VMEM)
SMEM = pl.BlockSpec(memory_space=pltpu.SMEM)
HBM = pl.BlockSpec(memory_space=pltpu.HBM)
PARAMS = pltpu.CompilerParams(vmem_limit_bytes=16 * 1024 * 1024)
F32 = jnp.float32


def swap(blocks, axis, spare):
    size, width = lax.axis_size(axis), lax.axis_size(spare)
    pairs = [(i, i ^ 1) for i in range(size)]
    axes = axis if isinstance(axis, tuple) else (axis,)
    ahead = ALL.index(spare) < ALL.index(axes[0])

    def at(i, k):
        return k * size + i if ahead else i * width + k

    others = []
    for i in range(size):
        j = ((i + 1) ^ 1) - 1
        for k in range(width):
            others.append((at(i, k), at(j, k) if 0 <= j < size else at(i, k ^ 1)))
    both = (spare, *axes) if ahead else (*axes, spare)
    near = lax.ppermute(blocks[0], axis, pairs)
    other = lax.ppermute(blocks[1], both, others)
    return near, other


def struct(*shape):
    return jax.ShapeDtypeStruct(shape, F32)


def in_hbm(array):
    return pltpu.with_memory_space_constraint(array, pltpu.HBM)


def presum(device, partials, code_bits, group_map, sizes, chunks):
    slots, nx, by, bz = partials.shape
    rows = nx // chunks

    def kernel(dev_ref, map_hbm, bits_hbm, part_ref, out_ref, buf, map_ref, bits_ref, sems):
        map_copy = pltpu.make_async_copy(map_hbm, map_ref, sems.at[chunks])
        bits_copy = pltpu.make_async_copy(bits_hbm, bits_ref, sems.at[chunks + 1])
        map_copy.start()
        bits_copy.start()

        def copy(c):
            part = pl.ds(c * rows, rows)
            return pltpu.make_async_copy(part_ref.at[:, part], buf.at[:, part], sems.at[c])

        for c in range(chunks):
            copy(c).start()
        map_copy.wait()
        bits_copy.wait()
        base = position(dev_ref, sizes)[0] * slots
        groups = [map_ref[base + s] for s in range(slots)]
        for c in range(chunks):
            copy(c).wait()

            def row(i, carry):
                x = c * rows + i
                total = None
                for s in range(slots):
                    sign = (2 * bits_ref[groups[s], x] - 1).astype(F32)
                    term = sign * buf[s, x]
                    total = term if total is None else total + term
                out_ref[x] = total
                return carry

            lax.fori_loop(0, rows, row, 0, unroll=4)

    return pl.pallas_call(
        kernel,
        name="presum",
        compiler_params=PARAMS,
        out_shape=struct(nx, by, bz),
        in_specs=[SMEM, HBM, HBM, HBM],
        out_specs=VMEM,
        scratch_shapes=[
            pltpu.VMEM(partials.shape, F32),
            pltpu.SMEM(group_map.shape, jnp.int32),
            pltpu.SMEM(code_bits.shape, jnp.int32),
            pltpu.SemaphoreType.DMA((chunks + 2,)),
        ],
    )(device, in_hbm(group_map), in_hbm(code_bits), in_hbm(partials))


def position(dev_ref, sizes):
    _, size_y, size_z = sizes
    dev = dev_ref[0]
    return dev // (size_y * size_z), (dev // size_z) % size_y, dev % size_z


def is_even(index):
    return index % 2 == 0


def reduce_pack(device, parts, velocity, sizes):
    bx, by, bz = velocity.shape
    members = sizes[0]

    def kernel(dev_ref, part_ref, v_ref, g_ref, near_ref, other_ref, square_ref):
        even = is_even(position(dev_ref, sizes)[0])
        squares = jnp.zeros((by, bz), F32)
        for i in range(bx):
            total = part_ref[i]
            for m in range(1, members):
                total = total + part_ref[m * bx + i]
            g_ref[i] = total
            squares = squares + total * total
        for i in range(HALO):
            for k, ref in enumerate((g_ref, v_ref)):
                first, last = ref[i], ref[bx - HALO + i]
                near_ref[k * HALO + i] = jnp.where(even, last, first)
                other_ref[k * HALO + i] = jnp.where(even, first, last)
        square_ref[...] = jnp.broadcast_to(jnp.sum(squares, axis=0, keepdims=True), (8, bz))

    edge = struct(2 * HALO, by, bz)
    return pl.pallas_call(
        kernel,
        name="reduce_pack",
        compiler_params=PARAMS,
        out_shape=(struct(bx, by, bz), edge, edge, struct(8, bz)),
        in_specs=[SMEM, VMEM, VMEM],
        out_specs=(VMEM,) * 4,
    )(device, parts, velocity)


def plane_of(main_ref, near_ref, other_ref, even, field, p):
    bx = main_ref.shape[0]
    if p < HALO:
        at = field * HALO + p
        return jnp.where(even, other_ref[at], near_ref[at])
    if p < HALO + bx:
        return main_ref[p - HALO]
    at = field * HALO + p - HALO - bx
    return jnp.where(even, near_ref[at], other_ref[at])


def sublane(shape):
    return lax.broadcasted_iota(jnp.int32, shape, len(shape) - 2)


def lane(shape):
    return lax.broadcasted_iota(jnp.int32, shape, len(shape) - 1)


def pack_y(device, gradient, velocity, halo_x, sizes):
    bx, by, bz = velocity.shape
    pairs = (bx + 2 * HALO) // 2

    def kernel(dev_ref, g_ref, v_ref, nx_ref, ox_ref, near_ref, other_ref):
        even_x, even_y = (is_even(i) for i in position(dev_ref, sizes)[:2])
        low = sublane((8, bz)) < 4
        for field, main in enumerate((g_ref, v_ref)):
            for q in range(pairs):
                left = plane_of(main, nx_ref, ox_ref, even_x, field, 2 * q)
                right = plane_of(main, nx_ref, ox_ref, even_x, field, 2 * q + 1)
                first = jnp.where(low, left[:8], pltpu.roll(right[:8], 4, 0))
                last = jnp.where(low, pltpu.roll(left[by - 8 :], 4, 0), right[by - 8 :])
                near_ref[field * pairs + q] = jnp.where(even_y, last, first)
                other_ref[field * pairs + q] = jnp.where(even_y, first, last)

    edge = struct(2 * pairs, 8, bz)
    return pl.pallas_call(
        kernel,
        name="pack_y",
        compiler_params=PARAMS,
        out_shape=(edge, edge),
        in_specs=[SMEM] + [VMEM] * 4,
        out_specs=(VMEM,) * 2,
    )(device, gradient, velocity, *halo_x)


def rows_of(near_ref, other_ref, even, field, p, pairs):
    near = near_ref[field * pairs + p // 2]
    other = other_ref[field * pairs + p // 2]
    low = sublane(near.shape) < 4
    after = jnp.where(even, near, other)
    before = jnp.where(even, other, near)
    if p % 2 == 0:
        return jnp.where(low, after, pltpu.roll(before, 4, 0))
    return jnp.where(low, pltpu.roll(after, 4, 0), before)


def pack_lanes(device, gradient, velocity, halo_x, sizes):
    bx, by, bz = velocity.shape
    planes = bx + 2 * HALO
    groups = bz // 4

    def kernel(dev_ref, g_ref, v_ref, nx_ref, ox_ref, first_ref, last_ref, near_ref, other_ref):
        even_x, even_y = (is_even(i) for i in position(dev_ref, sizes)[:2])
        group = lane((by, bz)) // 4
        for field, main in enumerate((g_ref, v_ref)):
            first = jnp.zeros((by, bz), F32)
            last = jnp.zeros((by, bz), F32)
            for p in range(planes):
                plane = plane_of(main, nx_ref, ox_ref, even_x, field, p)
                turned = pltpu.roll(plane, 4 * p, 1) if p else plane
                first = jnp.where(group == p, turned, first)
                last = jnp.where(group == (p - 1) % groups, turned, last)
            first_ref[pl.ds(field * by, by)] = first
            last_ref[pl.ds(field * by, by)] = last
            for k, packed in enumerate((first, last)):
                top, bottom = packed[:8], packed[by - 8 :]
                near_ref[2 * field + k] = jnp.where(even_y, bottom, top)
                other_ref[2 * field + k] = jnp.where(even_y, top, bottom)

    own = struct(2 * by, bz)
    edge = struct(4, 8, bz)
    return pl.pallas_call(
        kernel,
        name="pack_lanes",
        compiler_params=PARAMS,
        out_shape=(own, own, edge, edge),
        in_specs=[SMEM] + [VMEM] * 4,
        out_specs=(VMEM,) * 4,
    )(device, gradient, velocity, *halo_x)


def pack_z(device, first, last, corners, sizes):
    rows, bz = first.shape
    by = rows // 2
    tall = by + 8

    def kernel(dev_ref, first_ref, last_ref, nc_ref, oc_ref, near_ref, other_ref):
        even_y, even_z = (is_even(i) for i in position(dev_ref, sizes)[1:])
        low = sublane((8, bz)) < 4
        for field in range(2):
            both = []
            for k, ref in enumerate((first_ref, last_ref)):
                near, other = nc_ref[2 * field + k], oc_ref[2 * field + k]
                after = jnp.where(even_y, near, other)
                before = jnp.where(even_y, other, near)
                extra = jnp.where(low, after, before)
                both.append(jnp.concatenate([ref[pl.ds(field * by, by)], extra], 0))
            near_ref[pl.ds(field * tall, tall)] = jnp.where(even_z, both[1], both[0])
            other_ref[pl.ds(field * tall, tall)] = jnp.where(even_z, both[0], both[1])

    edge = struct(2 * tall, bz)
    return pl.pallas_call(
        kernel,
        name="pack_z",
        compiler_params=PARAMS,
        out_shape=(edge, edge),
        in_specs=[SMEM] + [VMEM] * 4,
        out_specs=(VMEM,) * 2,
    )(device, first, last, *corners)


def proximal(device, gradient, velocity, halos, squares, sizes):
    bx, by, bz = velocity.shape
    planes = bx + 2 * HALO
    pairs = planes // 2
    tall = by + 8
    wide = 2 * bz
    size_x, size_y, size_z = sizes
    cells = size_x * bx * size_y * by * size_z * bz

    def kernel(
        dev_ref,
        g_ref,
        v_ref,
        nx_ref,
        ox_ref,
        ny_ref,
        oy_ref,
        nz_ref,
        oz_ref,
        sq_ref,
        gradient_ref,
        model_ref,
        target,
        current,
        extra,
        dual_x,
        dual_y,
        dual_z,
        model,
        sems,
    ):
        gradient_copy = pltpu.make_async_copy(g_ref, gradient_ref, sems.at[0])
        gradient_copy.start()
        pos_x, pos_y, pos_z = position(dev_ref, sizes)
        even_x, even_y, even_z = (is_even(i) for i in (pos_x, pos_y, pos_z))

        total = jnp.sum(jnp.sum(sq_ref[...], axis=0), axis=1, keepdims=True)
        scale = step_length * lax.rsqrt(total / cells + 1.0)
        scale = jnp.broadcast_to(scale, (1, bz))

        side_lane = lane((tall, bz)) < bz // 2
        near_z = nz_ref[pl.ds(tall, tall)] - scale * nz_ref[pl.ds(0, tall)]
        other_z = oz_ref[pl.ds(tall, tall)] - scale * oz_ref[pl.ds(0, tall)]
        before_z = jnp.where(even_z, other_z, near_z)
        after_z = jnp.where(even_z, near_z, other_z)
        for p in range(planes):
            own, rows = (
                [
                    plane_of(main, nx_ref, ox_ref, even_x, field, p),
                    rows_of(ny_ref, oy_ref, even_y, field, p, pairs),
                ]
                for field, main in ((1, v_ref), (0, g_ref))
            )
            own, rows = (own[0] - scale * rows[0], own[1] - scale * rows[1])
            back = (bz - 4 * p) % bz
            after = pltpu.roll(after_z, back, 1) if back else after_z
            before = pltpu.roll(before_z, back, 1) if back else before_z
            target[p, pl.ds(0, by), pl.ds(0, bz)] = own
            target[p, pl.ds(by, 8), pl.ds(0, bz)] = rows
            target[p, :, pl.ds(bz, bz)] = jnp.where(side_lane, after, before)

        def factor(index, limit):
            return jnp.where((index >= 0) & (index < limit - 1), dual_step, 0.0).astype(F32)

        row = sublane((tall, 1))
        row = jnp.where(row < by + 4, row, row - tall) + pos_y * by
        factor_y = factor(row, size_y * by)
        col = lane((1, wide))
        col = jnp.where(col < bz + bz // 2, col, col - wide) + pos_z * bz
        factor_z = factor(col, size_z * bz)
        shrink = 1.0 / (1.0 + primal_step)
        gain = primal_step / (1.0 + primal_step)

        for iteration in range(ITERS):
            first = iteration == 0
            final = iteration == ITERS - 1
            here_ref = target if first else extra
            ahead = here_ref[iteration]
            before_x = None
            for p in range(iteration, planes - 1 - iteration):
                here = ahead
                ahead = here_ref[p + 1]
                index = pos_x * bx + (p - HALO)
                factor_x = factor(index, size_x * bx)
                dx = factor_x * (ahead - here)
                dy = factor_y * (pltpu.roll(here, tall - 1, 0) - here)
                dz = factor_z * (pltpu.roll(here, wide - 1, 1) - here)
                if not first:
                    dx = dual_x[p] + dx
                    dy = dual_y[p] + dy
                    dz = dual_z[p] + dz
                norm = dx * dx + dy * dy + dz * dz
                ratio = jnp.minimum(1.0, tv_weight * lax.rsqrt(norm))
                dx = dx * ratio
                dy = dy * ratio
                dz = dz * ratio
                if not final:
                    dual_x[p] = dx
                    dual_y[p] = dy
                    dual_z[p] = dz
                if p > iteration:
                    if final:
                        spread = dx[:by, :bz] - before_x
                        spread += dy[:by, :bz] - pltpu.roll(dy[:, :bz], 1, 0)[:by]
                        spread += dz[:by, :bz] - pltpu.roll(dz[:by], 1, 1)[:, :bz]
                        goal = target[p, pl.ds(0, by), pl.ds(0, bz)]
                        old = current[p, pl.ds(0, by), pl.ds(0, bz)]
                        model[p - HALO] = shrink * old + gain * (spread + goal)
                    else:
                        spread = dx - before_x
                        spread += dy - pltpu.roll(dy, 1, 0)
                        spread += dz - pltpu.roll(dz, 1, 1)
                        if first:
                            new = here + gain * spread
                            old = here
                        else:
                            old = current[p]
                            new = shrink * old + gain * (spread + target[p])
                        current[p] = new
                        extra[p] = 2.0 * new - old
                before_x = dx[:by, :bz] if final else dx
        model_copy = pltpu.make_async_copy(model, model_ref, sems.at[1])
        model_copy.start()
        gradient_copy.wait()
        model_copy.wait()

    field = pltpu.VMEM((planes, tall, wide), F32)
    return pl.pallas_call(
        kernel,
        name="proximal",
        compiler_params=PARAMS,
        out_shape=(struct(bx, by, bz),) * 2,
        in_specs=[SMEM] + [VMEM] * 9,
        out_specs=(HBM,) * 2,
        scratch_shapes=[field] * 6 + [pltpu.VMEM((bx, by, bz), F32), pltpu.SemaphoreType.DMA((2,))],
    )(device, gradient, velocity, *halos, squares)


def shards(partials, code_bits, group_map, velocity):
    sizes = tuple(lax.axis_size(axis) for axis in (GX, GY, "gz"))
    device = lax.axis_index(ALL).astype(jnp.int32).reshape(1)

    local = presum(device, partials, code_bits, group_map, sizes, 8)
    parts = lax.all_to_all(local, GX, split_axis=0, concat_axis=0, tiled=True)
    gradient, *send_x, squares = reduce_pack(device, parts, velocity, sizes)
    halo_x = swap(send_x, GX, GY[1])
    table = jnp.broadcast_to(
        squares[:1][None], (sizes[0] * sizes[1] * sizes[2], 1, squares.shape[1])
    )
    table = lax.all_to_all(table, ALL, split_axis=0, concat_axis=0, tiled=True)
    first, last, *send_corners = pack_lanes(device, gradient, velocity, halo_x, sizes)
    corners = swap(send_corners, GY, "gz")
    send_y = pack_y(device, gradient, velocity, halo_x, sizes)
    halo_y = swap(send_y, GY, "gz")

    send_z = pack_z(device, first, last, corners, sizes)
    halo_z = swap(send_z, "gz", GY[1])

    halos = (*halo_x, *halo_y, *halo_z)
    return proximal(device, gradient, velocity, halos, table, sizes)


def solution(mesh):
    torus = Mesh(
        mesh.devices.reshape(4, 2, 4, 2, mesh.shape["gz"]), ("gx_0", "gx_1", "gy_0", "gy_1", "gz")
    )
    placed = (P(GX, None, GY, "gz"), P(), P(), P(GX, GY, "gz"))
    return jax.shard_map(
        shards,
        mesh=torus,
        in_specs=placed,
        out_specs=(P(GX, GY, "gz"), P(GX, GY, "gz")),
        check_vma=False,
    )
```

profile of v0, /device:TPU:83, one launch (start us, length us, event | category | flops | bytes accessed | tf_op | source)
XLA Modules:
  0.0 59.4 jit_solution(14616451257666973366)
XLA Ops:
  0.6 0.0 copy-start
  0.7 2.4 %presum.1 = f32[128,16,128]{2,1,0:T(8,128)S(1)} custom-call(s32[1]{0:T(128)} %bitcast.dev_ref, s32[32]{0:T(128)} %map_hbm.1, s32[32,128]{1,0:T(8,128)} %bits_hbm.1, f32[4,128,16,128]{3,2,1,0:T(8,128)} %part_ref.1), custom_call_target="tpu_custom_call" | custom-call | tf_op jit(solution)/shard_map/presum/pallas_call | solution.py:90
  3.1 18.5 %all_to_all.10.part_ref = f32[128,16,128]{2,1,0:T(8,128)S(1)} all-to-all(f32[128,16,128]{2,1,0:T(8,128)S(1)} %presum.1), channel_id=1, replica_groups=mesh['gx_0'=4,'gx_1'=2,'gy_0'=4,'gy_1'=2,'gz'=4] {'gx_0','gx_1'}, dimensions={0} | all-to-all | bytes 2097152 | tf_op jit(solution)/shard_map/all_to_all | solution.py:412
  21.6 0.0 copy-done
  21.6 0.1 reduce_pack.1
  21.6 0.7 %broadcast_in_dim.9 = f32[256,1,128]{2,1,0:T(1,128)} broadcast(f32[128]{0:T(128)S(1)} %slice_bitcast_fusion), dimensions={2} | broadcast | bytes 131584 | tf_op jit(solution)/shard_map/broadcast_in_dim | solution.py:415
  22.4 14.4 %all-to-all-start.1 = ((f32[256,1,128]{2,1,0:T(1,128)}), f32[256,1,128]{2,1,0:T(1,128)S(1)}, u32[]{:S(2)}, u32[]{:S(2)}) async-start(f32[256,1,128]{2,1,0:T(1,128)} %broadcast_in_dim.9), calls=%async_computation.1 | async-start | bytes 262144 | tf_op jit(solution)/shard_map/all_to_all | solution.py:418
  36.8 1.5 %collective-permute-start = (f32[6,16,128]{2,1,0:T(8,128)S(1)}, f32[6,16,128]{2,1,0:T(8,128)S(1)}, u32[]{:S(2)}, u32[]{:S(2)}) collective-permute-start(f32[6,16,128]{2,1,0:T(8,128)S(1)} %get-tuple-element.15), channel_id=1, source_target_pairs={{0,32},{32,0},{64,96},{96,64},{128,160},{160,128},{192,224},{224,1... | collective-permute-start | bytes 147464 | tf_op jit(solution)/shard_map/ppermute | solution.py:42
  38.3 0.1 collective-permute-start.1
  38.4 2.1 %collective-permute-done.nx_ref = f32[6,16,128]{2,1,0:T(8,128)S(1)} collective-permute-done((f32[6,16,128]{2,1,0:T(8,128)S(1)}, f32[6,16,128]{2,1,0:T(8,128)S(1)}, u32[]{:S(2)}, u32[]{:S(2)}) %collective-permute-start) | collective-permute-done | bytes 49184 | tf_op jit(solution)/shard_map/ppermute | solution.py:42
  40.5 2.4 %collective-permute-done.1.ox_ref = f32[6,16,128]{2,1,0:T(8,128)S(1)} collective-permute-done((f32[6,16,128]{2,1,0:T(8,128)S(1)}, f32[6,16,128]{2,1,0:T(8,128)S(1)}, u32[]{:S(2)}, u32[]{:S(2)}) %collective-permute-start.1) | collective-permute-done | bytes 49184 | tf_op jit(solution)/shard_map/ppermute | solution.py:43
  42.9 1.3 %collective-permute-start.2 = (f32[22,8,128]{2,1,0:T(8,128)S(1)}, f32[22,8,128]{2,1,0:T(8,128)S(1)}, u32[]{:S(2)}, u32[]{:S(2)}) collective-permute-start(f32[22,8,128]{2,1,0:T(8,128)S(1)} %get-tuple-element.17), channel_id=1, source_target_pairs={{0,4},{4,0},{8,12},{12,8},{16,20},{20,16},{24,28},{28,24},{1,5},{5... | collective-permute-start | bytes 270344 | tf_op jit(solution)/shard_map/ppermute | solution.py:42
  44.2 2.8 %collective-permute-start.3 = (f32[22,8,128]{2,1,0:T(8,128)S(1)}, f32[22,8,128]{2,1,0:T(8,128)S(1)}, u32[]{:S(2)}, u32[]{:S(2)}) collective-permute-start(f32[22,8,128]{2,1,0:T(8,128)S(1)} %get-tuple-element.18), channel_id=1, source_target_pairs={{0,1},{1,0},{2,3},{3,2},{4,8},{5,9},{6,10},{7,11},{8,4},{9,5},{10,... | collective-permute-start | bytes 270344 | tf_op jit(solution)/shard_map/ppermute | solution.py:43
  47.0 0.2 pack_lanes.1
  47.2 0.1 collective-permute-start.4
  47.3 1.2 %collective-permute-start.5 = (f32[4,8,128]{2,1,0:T(8,128)S(1)}, f32[4,8,128]{2,1,0:T(8,128)S(1)}, u32[]{:S(2)}, u32[]{:S(2)}) collective-permute-start(f32[4,8,128]{2,1,0:T(8,128)S(1)} %get-tuple-element.22), channel_id=1, source_target_pairs={{0,1},{1,0},{2,3},{3,2},{4,8},{5,9},{6,10},{7,11},{8,4},{9,5},{10,... | collective-permute-start | bytes 49160 | tf_op jit(solution)/shard_map/ppermute | solution.py:43
  48.5 0.0 collective-permute-done.4.nc_ref
  48.5 4.2 %collective-permute-done.5.oc_ref = f32[4,8,128]{2,1,0:T(8,128)S(1)} collective-permute-done((f32[4,8,128]{2,1,0:T(8,128)S(1)}, f32[4,8,128]{2,1,0:T(8,128)S(1)}, u32[]{:S(2)}, u32[]{:S(2)}) %collective-permute-start.5) | collective-permute-done | bytes 16416 | tf_op jit(solution)/shard_map/ppermute | solution.py:43
  52.6 1.0 %collective-permute-start.6 = (f32[48,128]{1,0:T(8,128)S(1)}, f32[48,128]{1,0:T(8,128)S(1)}, u32[]{:S(2)}, u32[]{:S(2)}) collective-permute-start(f32[48,128]{1,0:T(8,128)S(1)} %get-tuple-element.23), channel_id=1, source_target_pairs={{0,1},{1,0},{2,3},{3,2},{4,5},{5,4},{6,7},{7,6},{8,9},{9,8},{10,11... | collective-permute-start | bytes 73736 | tf_op jit(solution)/shard_map/ppermute | solution.py:42
  53.7 0.0 collective-permute-start.7
  53.7 1.7 %collective-permute-done.6.nz_ref = f32[48,128]{1,0:T(8,128)S(1)} collective-permute-done((f32[48,128]{1,0:T(8,128)S(1)}, f32[48,128]{1,0:T(8,128)S(1)}, u32[]{:S(2)}, u32[]{:S(2)}) %collective-permute-start.6) | collective-permute-done | bytes 24608 | tf_op jit(solution)/shard_map/ppermute | solution.py:42
  55.4 1.4 %collective-permute-done.7.oz_ref = f32[48,128]{1,0:T(8,128)S(1)} collective-permute-done((f32[48,128]{1,0:T(8,128)S(1)}, f32[48,128]{1,0:T(8,128)S(1)}, u32[]{:S(2)}, u32[]{:S(2)}) %collective-permute-start.7) | collective-permute-done | bytes 24608 | tf_op jit(solution)/shard_map/ppermute | solution.py:43
  56.8 0.0 collective-permute-done.2.ny_ref
  56.8 0.0 collective-permute-done.3.oy_ref
  56.8 0.0 all-to-all-done.1.sq_ref
  56.8 2.6 %proximal.1 = (f32[16,16,128]{2,1,0:T(8,128)}, f32[16,16,128]{2,1,0:T(8,128)}) custom-call(s32[1]{0:T(128)} %bitcast.dev_ref, f32[16,16,128]{2,1,0:T(8,128)S(1)} %get-tuple-element.14.g_ref, f32[16,16,128]{2,1,0:T(8,128)S(1)} %copy-done, f32[6,16,128]{2,1,0:T(8,128)S(1)} %collective-permute-done.nx_ref, f32[6,16,128]{2,1,0:T(8,128)S(1)} %collective-permute-done.1.ox_ref, ...), custom_call_target="tpu_custom_call" | custom-call | tf_op jit(solution)/shard_map/proximal/pallas_call | solution.py:396
  (3 shorter events, 0.1 us)
Async XLA Ops:
  0.6 20.9 %copy-start = (f32[16,16,128]{2,1,0:T(8,128)S(1)}, f32[16,16,128]{2,1,0:T(8,128)}, u32[]{:S(2)}) copy-start(f32[16,16,128]{2,1,0:T(8,128)} %v_ref.7) | copy-start | bytes 393220
  22.4 34.4 %all-to-all-start.1 = ((f32[256,1,128]{2,1,0:T(1,128)}), f32[256,1,128]{2,1,0:T(1,128)S(1)}, u32[]{:S(2)}, u32[]{:S(2)}) async-start(f32[256,1,128]{2,1,0:T(1,128)} %broadcast_in_dim.9), calls=%async_computation.1 | async-start | bytes 262144 | tf_op jit(solution)/shard_map/all_to_all | solution.py:418
  36.8 3.7 %collective-permute-start = (f32[6,16,128]{2,1,0:T(8,128)S(1)}, f32[6,16,128]{2,1,0:T(8,128)S(1)}, u32[]{:S(2)}, u32[]{:S(2)}) collective-permute-start(f32[6,16,128]{2,1,0:T(8,128)S(1)} %get-tuple-element.15), channel_id=1, source_target_pairs={{0,32},{32,0},{64,96},{96,64},{128,160},{160,128},{192,224},{224,1... | collective-permute-start | bytes 147464 | tf_op jit(solution)/shard_map/ppermute | solution.py:42
  38.3 4.6 %collective-permute-start.1 = (f32[6,16,128]{2,1,0:T(8,128)S(1)}, f32[6,16,128]{2,1,0:T(8,128)S(1)}, u32[]{:S(2)}, u32[]{:S(2)}) collective-permute-start(f32[6,16,128]{2,1,0:T(8,128)S(1)} %get-tuple-element.16), channel_id=1, source_target_pairs={{0,4},{4,0},{32,64},{36,68},{64,32},{68,36},{96,128},{100,132},{12... | collective-permute-start | bytes 147464 | tf_op jit(solution)/shard_map/ppermute | solution.py:43
  42.9 13.9 %collective-permute-start.2 = (f32[22,8,128]{2,1,0:T(8,128)S(1)}, f32[22,8,128]{2,1,0:T(8,128)S(1)}, u32[]{:S(2)}, u32[]{:S(2)}) collective-permute-start(f32[22,8,128]{2,1,0:T(8,128)S(1)} %get-tuple-element.17), channel_id=1, source_target_pairs={{0,4},{4,0},{8,12},{12,8},{16,20},{20,16},{24,28},{28,24},{1,5},{5... | collective-permute-start | bytes 270344 | tf_op jit(solution)/shard_map/ppermute | solution.py:42
  44.2 12.6 %collective-permute-start.3 = (f32[22,8,128]{2,1,0:T(8,128)S(1)}, f32[22,8,128]{2,1,0:T(8,128)S(1)}, u32[]{:S(2)}, u32[]{:S(2)}) collective-permute-start(f32[22,8,128]{2,1,0:T(8,128)S(1)} %get-tuple-element.18), channel_id=1, source_target_pairs={{0,1},{1,0},{2,3},{3,2},{4,8},{5,9},{6,10},{7,11},{8,4},{9,5},{10,... | collective-permute-start | bytes 270344 | tf_op jit(solution)/shard_map/ppermute | solution.py:43
  47.2 1.3 %collective-permute-start.4 = (f32[4,8,128]{2,1,0:T(8,128)S(1)}, f32[4,8,128]{2,1,0:T(8,128)S(1)}, u32[]{:S(2)}, u32[]{:S(2)}) collective-permute-start(f32[4,8,128]{2,1,0:T(8,128)S(1)} %get-tuple-element.21), channel_id=1, source_target_pairs={{0,4},{4,0},{8,12},{12,8},{16,20},{20,16},{24,28},{28,24},{1,5},{5... | collective-permute-start | bytes 49160 | tf_op jit(solution)/shard_map/ppermute | solution.py:42
  47.3 5.4 %collective-permute-start.5 = (f32[4,8,128]{2,1,0:T(8,128)S(1)}, f32[4,8,128]{2,1,0:T(8,128)S(1)}, u32[]{:S(2)}, u32[]{:S(2)}) collective-permute-start(f32[4,8,128]{2,1,0:T(8,128)S(1)} %get-tuple-element.22), channel_id=1, source_target_pairs={{0,1},{1,0},{2,3},{3,2},{4,8},{5,9},{6,10},{7,11},{8,4},{9,5},{10,... | collective-permute-start | bytes 49160 | tf_op jit(solution)/shard_map/ppermute | solution.py:43
  52.6 2.8 %collective-permute-start.6 = (f32[48,128]{1,0:T(8,128)S(1)}, f32[48,128]{1,0:T(8,128)S(1)}, u32[]{:S(2)}, u32[]{:S(2)}) collective-permute-start(f32[48,128]{1,0:T(8,128)S(1)} %get-tuple-element.23), channel_id=1, source_target_pairs={{0,1},{1,0},{2,3},{3,2},{4,5},{5,4},{6,7},{7,6},{8,9},{9,8},{10,11... | collective-permute-start | bytes 73736 | tf_op jit(solution)/shard_map/ppermute | solution.py:42
  53.7 3.1 %collective-permute-start.7 = (f32[48,128]{1,0:T(8,128)S(1)}, f32[48,128]{1,0:T(8,128)S(1)}, u32[]{:S(2)}, u32[]{:S(2)}) collective-permute-start(f32[48,128]{1,0:T(8,128)S(1)} %get-tuple-element.24), channel_id=1, source_target_pairs={{0,4},{4,0},{1,2},{5,6},{2,1},{6,5},{3,7},{7,3},{8,12},{12,8},{9,1... | collective-permute-start | bytes 73736 | tf_op jit(solution)/shard_map/ppermute | solution.py:43
where the time goes:
time: 59.6 us; the launch traced here: 59.4 us
  starting transfers between devices  22.4 us (38%)
  blocking collectives  18.5 us (31%)
  waiting for transfers between devices  11.8 us (20%)
  Pallas kernels  5.28 us (9%)
  local copies, waits for them, and re-layouts  0.73 us (1%)
  between operations  0.71 us (1%)
    all_to_all x1, blocking collectives, shards(): parts = lax.all_to_all(local, GX, split_axis=0, concat_axis=0, tiled=True)  18.5 us
    all_to_all x1, starting transfers between devices, shards(): table = lax.all_to_all(table, ALL, split_axis=0, concat_axis=0, tiled=True)  14.4 us
    ppermute x4, waiting for transfers between devices, swap(): other = lax.ppermute(blocks[1], both, others)  7.96 us
    ppermute x4, starting transfers between devices, swap(): other = lax.ppermute(blocks[1], both, others)  4.11 us
    ppermute x4, starting transfers between devices, swap(): near = lax.ppermute(blocks[0], axis, pairs)  3.94 us
    ppermute x4, waiting for transfers between devices, swap(): near = lax.ppermute(blocks[0], axis, pairs)  3.8 us
    pallas_call x1, Pallas kernels, proximal(): pl.pallas_call(kernel, name='proximal', compiler_params=PARAMS, out_shape...  2.59 us
    pallas_call x1, Pallas kernels, presum(): pl.pallas_call(kernel, name='presum', compiler_params=PARAMS, out_shape=s...  2.43 us
  transfers between devices with their start and end apart: 9, of which 5 were waited for; matrix products, arithmetic and copies ran while one was open for 0% of the time, Pallas kernels for 0%

commit v1 on v0

--- a/solution.py
+++ b/solution.py
@@ -39,9 +39,7 @@
         for k in range(width):
             others.append((at(i, k), at(j, k) if 0 <= j < size else at(i, k ^ 1)))
     both = (spare, *axes) if ahead else (*axes, spare)
-    near = lax.ppermute(blocks[0], axis, pairs)
-    other = lax.ppermute(blocks[1], both, others)
-    return near, other
+    return lax.ppermute(blocks[0], axis, pairs), lax.ppermute(blocks[1], both, others)
 
 
 def struct(*shape):
@@ -85,7 +83,7 @@
                 out_ref[x] = total
                 return carry
 
-            lax.fori_loop(0, rows, row, 0, unroll=4)
+            lax.fori_loop(0, rows, row, 0, unroll=8)
 
     return pl.pallas_call(
         kernel,

time: 59.6 us -> 59.5 us (level)
  no operation moved by 1% of the time
where the time goes in v1:
time: 59.5 us; the launch traced here: 59.4 us
  starting transfers between devices  22.4 us (38%)
  blocking collectives  18.5 us (31%)
  waiting for transfers between devices  11.8 us (20%)
  Pallas kernels  5.26 us (9%)
  local copies, waits for them, and re-layouts  0.73 us (1%)
  between operations  0.71 us (1%)
    all_to_all x1, blocking collectives, shards(): parts = lax.all_to_all(local, GX, split_axis=0, concat_axis=0, tiled=True)  18.5 us
    all_to_all x1, starting transfers between devices, shards(): table = lax.all_to_all(table, ALL, split_axis=0, concat_axis=0, tiled=True)  14.4 us
    ppermute x4, waiting for transfers between devices, swap(): lax.ppermute(blocks[1], both, others)  7.96 us
    ppermute x4, starting transfers between devices, swap(): lax.ppermute(blocks[1], both, others)  4.11 us
    ppermute x4, starting transfers between devices, swap(): lax.ppermute(blocks[0], axis, pairs)  3.94 us
    ppermute x4, waiting for transfers between devices, swap(): lax.ppermute(blocks[0], axis, pairs)  3.8 us
    pallas_call x1, Pallas kernels, proximal(): pl.pallas_call(kernel, name='proximal', compiler_params=PARAMS, out_shape...  2.59 us
    pallas_call x1, Pallas kernels, presum(): pl.pallas_call(kernel, name='presum', compiler_params=PARAMS, out_shape=s...  2.41 us
  transfers between devices with their start and end apart: 9, of which 5 were waited for; matrix products, arithmetic and copies ran while one was open for 0% of the time, Pallas kernels for 0%

profile of v1, /device:TPU:83, one launch (start us, length us, event | category | flops | bytes accessed | tf_op | source)
XLA Modules:
  0.0 59.4 jit_solution(14655111371774476561)
XLA Ops:
  0.6 0.0 copy-start
  0.7 2.4 %presum.1 = f32[128,16,128]{2,1,0:T(8,128)S(1)} custom-call(s32[1]{0:T(128)} %bitcast.dev_ref, s32[32]{0:T(128)} %map_hbm.1, s32[32,128]{1,0:T(8,128)} %bits_hbm.1, f32[4,128,16,128]{3,2,1,0:T(8,128)} %part_ref.1), custom_call_target="tpu_custom_call" | custom-call | tf_op jit(solution)/shard_map/presum/pallas_call | solution.py:88
  3.1 18.5 %all_to_all.10.part_ref = f32[128,16,128]{2,1,0:T(8,128)S(1)} all-to-all(f32[128,16,128]{2,1,0:T(8,128)S(1)} %presum.1), channel_id=1, replica_groups=mesh['gx_0'=4,'gx_1'=2,'gy_0'=4,'gy_1'=2,'gz'=4] {'gx_0','gx_1'}, dimensions={0} | all-to-all | bytes 2097152 | tf_op jit(solution)/shard_map/all_to_all | solution.py:410
  21.5 0.0 copy-done
  21.5 0.1 reduce_pack.1
  21.6 0.7 %broadcast_in_dim.9 = f32[256,1,128]{2,1,0:T(1,128)} broadcast(f32[128]{0:T(128)S(1)} %slice_bitcast_fusion), dimensions={2} | broadcast | bytes 131584 | tf_op jit(solution)/shard_map/broadcast_in_dim | solution.py:413
  22.3 14.4 %all-to-all-start.1 = ((f32[256,1,128]{2,1,0:T(1,128)}), f32[256,1,128]{2,1,0:T(1,128)S(1)}, u32[]{:S(2)}, u32[]{:S(2)}) async-start(f32[256,1,128]{2,1,0:T(1,128)} %broadcast_in_dim.9), calls=%async_computation.1 | async-start | bytes 262144 | tf_op jit(solution)/shard_map/all_to_all | solution.py:416
  36.7 1.5 %collective-permute-start = (f32[6,16,128]{2,1,0:T(8,128)S(1)}, f32[6,16,128]{2,1,0:T(8,128)S(1)}, u32[]{:S(2)}, u32[]{:S(2)}) collective-permute-start(f32[6,16,128]{2,1,0:T(8,128)S(1)} %get-tuple-element.15), channel_id=1, source_target_pairs={{0,32},{32,0},{64,96},{96,64},{128,160},{160,128},{192,224},{224,1... | collective-permute-start | bytes 147464 | tf_op jit(solution)/shard_map/ppermute | solution.py:42
  38.3 0.1 collective-permute-start.1
  38.4 2.1 %collective-permute-done.nx_ref = f32[6,16,128]{2,1,0:T(8,128)S(1)} collective-permute-done((f32[6,16,128]{2,1,0:T(8,128)S(1)}, f32[6,16,128]{2,1,0:T(8,128)S(1)}, u32[]{:S(2)}, u32[]{:S(2)}) %collective-permute-start) | collective-permute-done | bytes 49184 | tf_op jit(solution)/shard_map/ppermute | solution.py:42
  40.4 2.4 %collective-permute-done.1.ox_ref = f32[6,16,128]{2,1,0:T(8,128)S(1)} collective-permute-done((f32[6,16,128]{2,1,0:T(8,128)S(1)}, f32[6,16,128]{2,1,0:T(8,128)S(1)}, u32[]{:S(2)}, u32[]{:S(2)}) %collective-permute-start.1) | collective-permute-done | bytes 49184 | tf_op jit(solution)/shard_map/ppermute | solution.py:42
  42.9 1.3 %collective-permute-start.2 = (f32[22,8,128]{2,1,0:T(8,128)S(1)}, f32[22,8,128]{2,1,0:T(8,128)S(1)}, u32[]{:S(2)}, u32[]{:S(2)}) collective-permute-start(f32[22,8,128]{2,1,0:T(8,128)S(1)} %get-tuple-element.17), channel_id=1, source_target_pairs={{0,4},{4,0},{8,12},{12,8},{16,20},{20,16},{24,28},{28,24},{1,5},{5... | collective-permute-start | bytes 270344 | tf_op jit(solution)/shard_map/ppermute | solution.py:42
  44.2 2.8 %collective-permute-start.3 = (f32[22,8,128]{2,1,0:T(8,128)S(1)}, f32[22,8,128]{2,1,0:T(8,128)S(1)}, u32[]{:S(2)}, u32[]{:S(2)}) collective-permute-start(f32[22,8,128]{2,1,0:T(8,128)S(1)} %get-tuple-element.18), channel_id=1, source_target_pairs={{0,1},{1,0},{2,3},{3,2},{4,8},{5,9},{6,10},{7,11},{8,4},{9,5},{10,... | collective-permute-start | bytes 270344 | tf_op jit(solution)/shard_map/ppermute | solution.py:42
  47.0 0.2 pack_lanes.1
  47.1 0.1 collective-permute-start.4
  47.2 1.2 %collective-permute-start.5 = (f32[4,8,128]{2,1,0:T(8,128)S(1)}, f32[4,8,128]{2,1,0:T(8,128)S(1)}, u32[]{:S(2)}, u32[]{:S(2)}) collective-permute-start(f32[4,8,128]{2,1,0:T(8,128)S(1)} %get-tuple-element.22), channel_id=1, source_target_pairs={{0,1},{1,0},{2,3},{3,2},{4,8},{5,9},{6,10},{7,11},{8,4},{9,5},{10,... | collective-permute-start | bytes 49160 | tf_op jit(solution)/shard_map/ppermute | solution.py:42
  48.4 0.0 collective-permute-done.4.nc_ref
  48.4 4.2 %collective-permute-done.5.oc_ref = f32[4,8,128]{2,1,0:T(8,128)S(1)} collective-permute-done((f32[4,8,128]{2,1,0:T(8,128)S(1)}, f32[4,8,128]{2,1,0:T(8,128)S(1)}, u32[]{:S(2)}, u32[]{:S(2)}) %collective-permute-start.5) | collective-permute-done | bytes 16416 | tf_op jit(solution)/shard_map/ppermute | solution.py:42
  52.6 1.0 %collective-permute-start.6 = (f32[48,128]{1,0:T(8,128)S(1)}, f32[48,128]{1,0:T(8,128)S(1)}, u32[]{:S(2)}, u32[]{:S(2)}) collective-permute-start(f32[48,128]{1,0:T(8,128)S(1)} %get-tuple-element.23), channel_id=1, source_target_pairs={{0,1},{1,0},{2,3},{3,2},{4,5},{5,4},{6,7},{7,6},{8,9},{9,8},{10,11... | collective-permute-start | bytes 73736 | tf_op jit(solution)/shard_map/ppermute | solution.py:42
  53.7 0.0 collective-permute-start.7
  53.7 1.7 %collective-permute-done.6.nz_ref = f32[48,128]{1,0:T(8,128)S(1)} collective-permute-done((f32[48,128]{1,0:T(8,128)S(1)}, f32[48,128]{1,0:T(8,128)S(1)}, u32[]{:S(2)}, u32[]{:S(2)}) %collective-permute-start.6) | collective-permute-done | bytes 24608 | tf_op jit(solution)/shard_map/ppermute | solution.py:42
  55.4 1.4 %collective-permute-done.7.oz_ref = f32[48,128]{1,0:T(8,128)S(1)} collective-permute-done((f32[48,128]{1,0:T(8,128)S(1)}, f32[48,128]{1,0:T(8,128)S(1)}, u32[]{:S(2)}, u32[]{:S(2)}) %collective-permute-start.7) | collective-permute-done | bytes 24608 | tf_op jit(solution)/shard_map/ppermute | solution.py:42
  56.8 0.0 collective-permute-done.2.ny_ref
  56.8 0.0 collective-permute-done.3.oy_ref
  56.8 0.0 all-to-all-done.1.sq_ref
  56.8 2.6 %proximal.1 = (f32[16,16,128]{2,1,0:T(8,128)}, f32[16,16,128]{2,1,0:T(8,128)}) custom-call(s32[1]{0:T(128)} %bitcast.dev_ref, f32[16,16,128]{2,1,0:T(8,128)S(1)} %get-tuple-element.14.g_ref, f32[16,16,128]{2,1,0:T(8,128)S(1)} %copy-done, f32[6,16,128]{2,1,0:T(8,128)S(1)} %collective-permute-done.nx_ref, f32[6,16,128]{2,1,0:T(8,128)S(1)} %collective-permute-done.1.ox_ref, ...), custom_call_target="tpu_custom_call" | custom-call | tf_op jit(solution)/shard_map/proximal/pallas_call | solution.py:394
  (3 shorter events, 0.1 us)
Async XLA Ops:
  0.6 20.9 %copy-start = (f32[16,16,128]{2,1,0:T(8,128)S(1)}, f32[16,16,128]{2,1,0:T(8,128)}, u32[]{:S(2)}) copy-start(f32[16,16,128]{2,1,0:T(8,128)} %v_ref.7) | copy-start | bytes 393220
  22.3 34.4 %all-to-all-start.1 = ((f32[256,1,128]{2,1,0:T(1,128)}), f32[256,1,128]{2,1,0:T(1,128)S(1)}, u32[]{:S(2)}, u32[]{:S(2)}) async-start(f32[256,1,128]{2,1,0:T(1,128)} %broadcast_in_dim.9), calls=%async_computation.1 | async-start | bytes 262144 | tf_op jit(solution)/shard_map/all_to_all | solution.py:416
  36.7 3.7 %collective-permute-start = (f32[6,16,128]{2,1,0:T(8,128)S(1)}, f32[6,16,128]{2,1,0:T(8,128)S(1)}, u32[]{:S(2)}, u32[]{:S(2)}) collective-permute-start(f32[6,16,128]{2,1,0:T(8,128)S(1)} %get-tuple-element.15), channel_id=1, source_target_pairs={{0,32},{32,0},{64,96},{96,64},{128,160},{160,128},{192,224},{224,1... | collective-permute-start | bytes 147464 | tf_op jit(solution)/shard_map/ppermute | solution.py:42
  38.3 4.6 %collective-permute-start.1 = (f32[6,16,128]{2,1,0:T(8,128)S(1)}, f32[6,16,128]{2,1,0:T(8,128)S(1)}, u32[]{:S(2)}, u32[]{:S(2)}) collective-permute-start(f32[6,16,128]{2,1,0:T(8,128)S(1)} %get-tuple-element.16), channel_id=1, source_target_pairs={{0,4},{4,0},{32,64},{36,68},{64,32},{68,36},{96,128},{100,132},{12... | collective-permute-start | bytes 147464 | tf_op jit(solution)/shard_map/ppermute | solution.py:42
  42.9 13.9 %collective-permute-start.2 = (f32[22,8,128]{2,1,0:T(8,128)S(1)}, f32[22,8,128]{2,1,0:T(8,128)S(1)}, u32[]{:S(2)}, u32[]{:S(2)}) collective-permute-start(f32[22,8,128]{2,1,0:T(8,128)S(1)} %get-tuple-element.17), channel_id=1, source_target_pairs={{0,4},{4,0},{8,12},{12,8},{16,20},{20,16},{24,28},{28,24},{1,5},{5... | collective-permute-start | bytes 270344 | tf_op jit(solution)/shard_map/ppermute | solution.py:42
  44.2 12.6 %collective-permute-start.3 = (f32[22,8,128]{2,1,0:T(8,128)S(1)}, f32[22,8,128]{2,1,0:T(8,128)S(1)}, u32[]{:S(2)}, u32[]{:S(2)}) collective-permute-start(f32[22,8,128]{2,1,0:T(8,128)S(1)} %get-tuple-element.18), channel_id=1, source_target_pairs={{0,1},{1,0},{2,3},{3,2},{4,8},{5,9},{6,10},{7,11},{8,4},{9,5},{10,... | collective-permute-start | bytes 270344 | tf_op jit(solution)/shard_map/ppermute | solution.py:42
  47.1 1.3 %collective-permute-start.4 = (f32[4,8,128]{2,1,0:T(8,128)S(1)}, f32[4,8,128]{2,1,0:T(8,128)S(1)}, u32[]{:S(2)}, u32[]{:S(2)}) collective-permute-start(f32[4,8,128]{2,1,0:T(8,128)S(1)} %get-tuple-element.21), channel_id=1, source_target_pairs={{0,4},{4,0},{8,12},{12,8},{16,20},{20,16},{24,28},{28,24},{1,5},{5... | collective-permute-start | bytes 49160 | tf_op jit(solution)/shard_map/ppermute | solution.py:42
  47.2 5.4 %collective-permute-start.5 = (f32[4,8,128]{2,1,0:T(8,128)S(1)}, f32[4,8,128]{2,1,0:T(8,128)S(1)}, u32[]{:S(2)}, u32[]{:S(2)}) collective-permute-start(f32[4,8,128]{2,1,0:T(8,128)S(1)} %get-tuple-element.22), channel_id=1, source_target_pairs={{0,1},{1,0},{2,3},{3,2},{4,8},{5,9},{6,10},{7,11},{8,4},{9,5},{10,... | collective-permute-start | bytes 49160 | tf_op jit(solution)/shard_map/ppermute | solution.py:42
  52.6 2.8 %collective-permute-start.6 = (f32[48,128]{1,0:T(8,128)S(1)}, f32[48,128]{1,0:T(8,128)S(1)}, u32[]{:S(2)}, u32[]{:S(2)}) collective-permute-start(f32[48,128]{1,0:T(8,128)S(1)} %get-tuple-element.23), channel_id=1, source_target_pairs={{0,1},{1,0},{2,3},{3,2},{4,5},{5,4},{6,7},{7,6},{8,9},{9,8},{10,11... | collective-permute-start | bytes 73736 | tf_op jit(solution)/shard_map/ppermute | solution.py:42
  53.7 3.1 %collective-permute-start.7 = (f32[48,128]{1,0:T(8,128)S(1)}, f32[48,128]{1,0:T(8,128)S(1)}, u32[]{:S(2)}, u32[]{:S(2)}) collective-permute-start(f32[48,128]{1,0:T(8,128)S(1)} %get-tuple-element.24), channel_id=1, source_target_pairs={{0,4},{4,0},{1,2},{5,6},{2,1},{6,5},{3,7},{7,3},{8,12},{12,8},{9,1... | collective-permute-start | bytes 73736 | tf_op jit(solution)/shard_map/ppermute | solution.py:42
